TPU v7x, 8 devices: a whole 2x2x1 slice. The times are simulated.
8 devices in a mesh: dp: 1 (over z), tp: 2 (over y), ep: 4 (over x, core).
Axes of the slice: x: 2, y: 2, z: 1, core: 2. Of those that a mesh axis runs over, the one named last changes fastest.
Arguments:
- normed: bfloat16 [2048, 2048], P(('dp', 'ep'))
- residual: bfloat16 [2048, 2048], P(('dp', 'ep'))
- w_router: float32 [2048, 60], replicated
- ws_gate: bfloat16 [2048, 5632], P(None, 'tp')
- ws_up: bfloat16 [2048, 5632], P(None, 'tp')
- ws_down: bfloat16 [5632, 2048], P('tp')
- we_gate: bfloat16 [60, 2048, 1408], P('ep', None, 'tp')
- we_up: bfloat16 [60, 2048, 1408], P('ep', None, 'tp')
- we_down: bfloat16 [60, 1408, 2048], P('ep', 'tp')
- first_id: int32 [2048], P(('dp', 'ep'))
- alt_id: int32 [2048], P(('dp', 'ep'))
Outputs:
- output: bfloat16 [2048, 2048], P(('dp', 'ep'))
All inputs are finite; a program needn't handle non-finite values.
Results may differ from a plain program's by a relative error of at most 0.00530088.
Values are sent between devices in bfloat16 or wider.
A program may use at most 1 GiB of HBM per device.

v0:
```python
import functools

import jax
import jax.numpy as jnp
from jax import lax
from jax.experimental import pallas as pl
from jax.experimental.pallas import tpu as pltpu
from jax.sharding import PartitionSpec as P

MESH = pl.DeviceIdType.MESH
F32 = jnp.float32
BF16 = jnp.bfloat16
LANES = 128
RANK_BLOCK = 256
X_SPLIT = (0, 192, 320, 448, 512)
X_CHUNKS = 4
WIDE = 512
COPY_CHUNKS = 4
ROW_BLOCKS = 2
COL = 256
SUBS = 2
EARLY_GROUPS = 4
SHARED_BUFS = 4


def dot(a, b):
    return jnp.dot(a, b, preferred_element_type=F32)


def dot_bt(a, b):
    return lax.dot_general(a, b, (((1,), (1,)), ((), ())), preferred_element_type=F32)


def dot_at(a, b):
    return lax.dot_general(a, b, (((0,), (0,)), ((), ())), preferred_element_type=F32)


def moe_kernel(dims, x_hbm, res_hbm, wr_hbm, wsg_hbm, wsu_hbm, wsd_hbm, weg_hbm, weu_hbm, wed_hbm, first_ref, alt_ref, o_hbm,
               x_near, x_far, x_sorted, ids_all, code_rows, code_col, gate_col, slot_x, sh_own, sh_send, sh_recv, ex_own, ex_send, ex_recv, ret, out_half, res_half, wr,
               ld_sem, id_send, id_recv, sib_send, sib_recv, xp_send, xp_recv, fw_send, fw_recv,
               ysh_send, ysh_recv, yex_send, yex_recv, rs_send, rs_recv, rx_send, rx_recv, rf_send, rf_recv, yo_send, yo_recv, lo_sem):
    experts, capacity, window, pack, bounds, local_experts, ep_size = dims
    groups = len(bounds) - 1
    last_expert = [-(-min(b, local_experts * capacity) // capacity) - 1 for b in bounds[1:]]
    tok, d_model = x_hbm.shape
    half = d_model // 2
    slots = local_experts * window
    spare = pack - local_experts * capacity
    ff_shared = wsg_hbm.shape[1]
    ff_expert = weg_hbm.shape[1]
    dp = lax.axis_index("dp")
    t = lax.axis_index("tp")
    me = lax.axis_index("ep")
    core = lax.rem(me, 2)
    sib = me + 1 - 2 * core
    xp = lax.rem(me + 2, ep_size)
    diag = lax.rem(sib + 2, ep_size)
    y_peer = (dp, 1 - t, me)
    sib_dev = (dp, t, sib)
    xp_dev = (dp, t, xp)
    diag_dev = (dp, t, diag)
    own_off = pl.multiple_of(t * half, half)
    peer_off = pl.multiple_of((1 - t) * half, half)
    x_cuts = [tok * v // X_SPLIT[-1] for v in X_SPLIT]
    r_rows = tok // ROW_BLOCKS
    n_wide, tail = ff_shared // WIDE, ff_shared % WIDE
    n_chunks = n_wide + (tail > 0)
    n_half = half // WIDE
    sub_cols = half // SUBS
    sub_blocks = sub_cols // WIDE
    sent = -(-local_experts * capacity // 8) * 8

    barrier = pltpu.get_barrier_semaphore()
    for dev in (y_peer, sib_dev, xp_dev, diag_dev):
        pl.semaphore_signal(barrier, inc=1, device_id=dev, device_id_type=MESH)

    def remote(src, dst, s_sem, r_sem, dev):
        return pltpu.make_async_remote_copy(src_ref=src, dst_ref=dst, send_sem=s_sem, recv_sem=r_sem, device_id=dev, device_id_type=MESH)

    id_copies = [remote(ids_all.at[me], ids_all.at[me], id_send.at[i], id_recv.at[i], dev) for i, dev in enumerate((sib_dev, xp_dev, diag_dev))]
    def far_rows(c, i):
        n = x_cuts[c + 1] - x_cuts[c]
        return pl.ds(2 * x_cuts[c] + i * n, n)

    xp_copies = [remote(x_sorted.at[pl.ds(x_cuts[c], x_cuts[c + 1] - x_cuts[c])], x_far.at[far_rows(c, 0)], xp_send.at[c], xp_recv.at[c], xp_dev) for c in range(X_CHUNKS)]
    sib_copy = remote(x_near.at[0], x_near.at[1], sib_send.at[0], sib_recv.at[0], sib_dev)
    fw_copies = [remote(x_far.at[far_rows(c, 0)], x_far.at[far_rows(c, 1)], fw_send.at[c], fw_recv.at[c], sib_dev) for c in range(X_CHUNKS)]
    own_x = [pltpu.make_async_copy(x_hbm.at[pl.ds(r * r_rows, r_rows)], x_near.at[0, pl.ds(r * r_rows, r_rows)], ld_sem.at[r]) for r in range(ROW_BLOCKS)]
    res_load = pltpu.make_async_copy(res_hbm.at[:, pl.ds(own_off, half)], res_half, ld_sem.at[ROW_BLOCKS])
    wr_load = pltpu.make_async_copy(wr_hbm, wr, ld_sem.at[ROW_BLOCKS + 1])

    cap = jnp.float32(capacity)

    def expert_base(ids):
        owner = sum((ids >= q * local_experts).astype(jnp.int32) for q in range(1, ep_size))
        return (ids * capacity + owner * spare).astype(F32)

    def route():
        for copy in id_copies:
            copy.wait()
        e_pad = -(-experts // 8) * 8
        e_iota = lax.broadcasted_iota(jnp.int32, (e_pad, RANK_BLOCK), 0)
        row_i = lax.broadcasted_iota(jnp.int32, (RANK_BLOCK, RANK_BLOCK), 0)
        col_i = lax.broadcasted_iota(jnp.int32, (RANK_BLOCK, RANK_BLOCK), 1)
        upper = (row_i <= col_i).astype(F32).astype(BF16)
        blocks = [(q, b * RANK_BLOCK) for q in range(ep_size) for b in range(tok // RANK_BLOCK)]
        total = jnp.zeros((e_pad, 1), F32)
        rank_first = []
        for q, lo in blocks:
            first = ids_all[q, 0:1, lo:lo + RANK_BLOCK]
            hot = (e_iota == first).astype(F32)
            cum = dot(hot.astype(BF16), upper) + total
            rank_first.append(jnp.sum(cum * hot, axis=0, keepdims=True) - 1.0)
            total = total + jnp.sum(hot, axis=1, keepdims=True)
        load = jnp.minimum(total, cap)
        room = cap - load
        total = jnp.zeros((e_pad, 1), F32)
        for i, (q, lo) in enumerate(blocks):
            first = ids_all[q, 0:1, lo:lo + RANK_BLOCK]
            alt = ids_all[q, 1:2, lo:lo + RANK_BLOCK]
            kept = rank_first[i] < cap
            over = jnp.where(kept, 0.0, 1.0)
            hot = (e_iota == alt).astype(F32) * over
            cum = dot(hot.astype(BF16), upper) + total
            rank_alt = jnp.sum(cum * hot, axis=0, keepdims=True) - 1.0
            total = total + jnp.sum(hot, axis=1, keepdims=True)
            room_tok = jnp.sum(hot * room, axis=0, keepdims=True)
            load_tok = jnp.sum(hot * load, axis=0, keepdims=True)
            code_first = expert_base(first) + rank_first[i]
            code_alt = jnp.where(rank_alt < room_tok, expert_base(alt) + load_tok + rank_alt, -1.0)
            code = jnp.where(kept, code_first, code_alt)
            code_rows[q, :, lo:lo + RANK_BLOCK] = jnp.broadcast_to(code, (8, RANK_BLOCK))

    def sort_block(q):
        code_t = jnp.broadcast_to(code_rows[q][0:1, :], (LANES, tok)).T[:, 0:1]
        shift = ((1 - lax.div(q, 2)) * (2 * pack)).astype(F32)

        def key_of(code):
            rel = code - shift
            local = jnp.where(rel >= pack, rel - pack, rel)
            return jnp.where((rel >= 0.0) & (rel < 2.0 * pack), local, 8192.0)

        key_t = key_of(code_t)
        key = key_of(code_rows[q][0:1, :])
        lane = lax.broadcasted_iota(jnp.int32, (tok, tok), 1)
        line = lax.broadcasted_iota(jnp.int32, (tok, tok), 0)
        ahead = (key < key_t) | ((key == key_t) & (lane < line))
        position = jnp.sum(jnp.where(ahead, 1.0, 0.0), axis=1, keepdims=True)
        return position == lane.astype(F32), code_t

    def dispatch():
        route()
        hit, _ = sort_block(me)
        order = hit.astype(F32).astype(BF16)
        for lo in range(0, d_model, WIDE):
            x_sorted[:, lo:lo + WIDE] = dot_at(order, x_near[0, :, lo:lo + WIDE]).astype(BF16)
        xp_copies[0].start()

    def ysh_copy(r, j):
        if r == 0:
            return remote(sh_send.at[r, j], sh_recv.at[r, j], ysh_send.at[r, j], ysh_recv.at[r, j], y_peer)
        return remote(sh_send.at[r], sh_recv.at[r], ysh_send.at[r, 0], ysh_recv.at[r, 0], y_peer)

    def shared_phase(act, wg, wu, wd, g_sem, u_sem, d_sem):
        def weight_copies(c, slot, width):
            cols = pl.ds(pl.multiple_of(c * WIDE, WIDE), width)
            dst = pl.ds(0, width)
            return (pltpu.make_async_copy(wsg_hbm.at[:, cols], wg.at[slot, :, dst], g_sem.at[slot]),
                    pltpu.make_async_copy(wsu_hbm.at[:, cols], wu.at[slot, :, dst], u_sem.at[slot]))

        def start_weights(k, slot):
            c = lax.rem(k, n_chunks)

            @pl.when(c < n_wide)
            def _():
                for copy in weight_copies(c, slot, WIDE):
                    copy.start()

            if tail:
                @pl.when(c == n_wide)
                def _():
                    for copy in weight_copies(c, slot, tail):
                        copy.start()

        def down_copy(k, slot):
            j = lax.rem(k, 2 * n_half)
            col = jnp.where(j < n_half, peer_off + j * WIDE, own_off + (j - n_half) * WIDE)
            return pltpu.make_async_copy(wsd_hbm.at[:, pl.ds(pl.multiple_of(col, WIDE), WIDE)], wd.at[slot], d_sem.at[slot])

        own_x[0].start()
        start_weights(jnp.int32(0), 0)
        for copy in own_x[1:]:
            copy.start()
        for slot in range(1, SHARED_BUFS):
            start_weights(jnp.int32(slot), slot)
        ids_all[pl.ds(me, 1), 0:1, :] = first_ref[...].reshape(1, 1, tok)
        ids_all[pl.ds(me, 1), 1:2, :] = alt_ref[...].reshape(1, 1, tok)
        def exchange():
            for copy in own_x[1:]:
                copy.wait()
            pl.semaphore_wait(barrier, 4)
            for copy in id_copies:
                copy.start()
            sib_copy.start()

        for r in range(ROW_BLOCKS):
            if r == 0:
                own_x[0].wait()
            def gateup(c, width):
                k = c + r * n_chunks
                slot = lax.rem(k, SHARED_BUFS)
                for copy in weight_copies(c, slot, width):
                    copy.wait()
                x = x_near[0, r * r_rows:(r + 1) * r_rows, :]
                for lo in range(0, width, COL):
                    g = dot(x, wg[slot, :, lo:lo + COL])
                    u = dot(x, wu[slot, :, lo:lo + COL])
                    act[:, pl.ds(pl.multiple_of(c * WIDE + lo, COL), COL)] = (jax.nn.silu(g) * u).astype(BF16)

                @pl.when(k + SHARED_BUFS < (r + 1) * n_chunks)
                def _():
                    start_weights(k + SHARED_BUFS, slot)

            with jax.named_scope(f"gateup{r}"):
                @pl.loop(0, n_wide)
                def _(c):
                    gateup(c, WIDE)

                    if r == 0:
                        @pl.when(c == 0)
                        def _():
                            exchange()

                    if r == 0:
                        @pl.when((c == 1) | (c == 3))
                        def _():
                            slot = lax.div(c, 2)
                            down_copy(slot, slot).start()

                if tail:
                    gateup(jnp.int32(n_wide), tail)

            if r + 1 < ROW_BLOCKS:
                for i in range(SHARED_BUFS):
                    k = (r + 1) * n_chunks + i
                    start_weights(jnp.int32(k), k % SHARED_BUFS)

            def down(j, base, store):
                k = j + r * 2 * n_half + base
                slot = lax.rem(k, 2)
                down_copy(k, slot).wait()
                store(dot(act[...], wd[slot]))

                @pl.when(k + 2 < ROW_BLOCKS * 2 * n_half)
                def _():
                    down_copy(k + 2, slot).start()

            with jax.named_scope(f"downpeer{r}"):
                @pl.loop(0, n_half)
                def _(j):
                    def store(value):
                        sh_send[r, j] = value
                        if r == 0:
                            ysh_copy(r, j).start()

                    down(j, 0, store)

                if r > 0:
                    ysh_copy(r, 0).start()

            if r == 0:
                wr_load.start()
                with jax.named_scope("dispatch"):
                    dispatch()
            with jax.named_scope(f"downown{r}"):
                @pl.loop(0, n_half)
                def _(j):
                    def store(value):
                        sh_own[j, r * r_rows:(r + 1) * r_rows, :] = value

                    down(j, n_half, store)

    shared_sems = [pltpu.SemaphoreType.DMA((SHARED_BUFS,))] * 3
    pl.run_scoped(shared_phase, pltpu.VMEM((r_rows, ff_shared), BF16), pltpu.VMEM((SHARED_BUFS, d_model, WIDE), BF16), pltpu.VMEM((SHARED_BUFS, d_model, WIDE), BF16),
                  pltpu.VMEM((2, ff_shared, WIDE), BF16), *shared_sems)

    def yex_copy(sub, i):
        rows = pl.ds(bounds[i], min(bounds[i + 1], sent) - bounds[i])
        return remote(ex_send.at[sub, rows], ex_recv.at[sub, rows], yex_send.at[sub, i], yex_recv.at[sub, i], y_peer)

    def ret_copy(sub, i, who, s_sem, r_sem, dev):
        ref = ret.at[sub, who, pl.ds(bounds[i], bounds[i + 1] - bounds[i])]
        return remote(ref, ref, s_sem.at[sub, i], r_sem.at[sub, i], dev)

    def give(sub, i):
        yex_copy(sub, i).wait()
        rows = slice(bounds[i], bounds[i + 1])
        ret[sub, pl.ds(me, 1), rows, :] = (ex_own[sub, rows, :] + ex_recv[sub, rows, :]).astype(BF16).reshape(1, bounds[i + 1] - bounds[i], sub_cols)
        ret_copy(sub, i, me, rx_send, rx_recv, xp_dev).start()
        ret_copy(sub, i, me, rs_send, rs_recv, sib_dev).start()

    def forward(sub, i):
        ret_copy(sub, i, me, rx_send, rx_recv, xp_dev).wait()
        ret_copy(sub, i, xp, rf_send, rf_recv, sib_dev).start()

    def routed_phase(sel_near, sel_far, wg, wu, wd, g_sem, u_sem, d_sem):
        def gate_copy(e, slot):
            return pltpu.make_async_copy(weg_hbm.at[e], wg.at[slot], g_sem.at[slot])

        def up_copy(e, slot):
            return pltpu.make_async_copy(weu_hbm.at[e], wu.at[slot], u_sem.at[slot])

        def down_copy(e, slot):
            return pltpu.make_async_copy(wed_hbm.at[e], wd.at[slot], d_sem.at[slot])

        for slot in range(2):
            gate_copy(slot, slot).start()
            up_copy(slot, slot).start()
            down_copy(slot, slot).start()

        res_load.start()
        xp_copies[1].start()
        with jax.named_scope("routing"):
            pos = lax.broadcasted_iota(jnp.int32, (slots, LANES), 0)
            slot_expert = sum((pos >= e * window).astype(jnp.int32) for e in range(1, local_experts))
            first_row = slot_expert * capacity
            row = (first_row // 8) * 8 + (pos - slot_expert * window)
            slot_code = jnp.where((row >= first_row) & (row < first_row + capacity), row + me * pack, -2).astype(F32)
            def pick_rows(codes):
                return (jnp.broadcast_to(slot_code[:, 0:1], (slots, codes.shape[1])) == codes).astype(F32).astype(BF16)

            for i, q in enumerate((me, sib)):
                codes = code_rows[q]
                for lo in range(0, tok, LANES):
                    sel_near[:, i * tok + lo:i * tok + lo + LANES] = pick_rows(codes[0:1, lo:lo + LANES])
            def sorted_codes(q):
                hit, code_t = sort_block(q)
                return jnp.sum(jnp.where(hit, code_t, 0.0), axis=0, keepdims=True)

            codes_xp, codes_diag = sorted_codes(xp), sorted_codes(diag)
            for c in range(X_CHUNKS):
                both = jnp.concatenate([codes_xp[:, x_cuts[c]:x_cuts[c + 1]], codes_diag[:, x_cuts[c]:x_cuts[c + 1]]], axis=1)
                for lo in range(0, 2 * (x_cuts[c + 1] - x_cuts[c]), LANES):
                    dst = 2 * x_cuts[c] + lo
                    sel_far[:, dst:dst + LANES] = pick_rows(both[:, lo:lo + LANES])

            code_t = jnp.broadcast_to(code_rows[me][0:1, :], (LANES, tok)).T
            code_col[...] = code_t

        nc = 512
        with jax.named_scope("near"):
            sib_copy.wait()

            @pl.loop(0, d_model // nc)
            def _(n):
                cols = pl.ds(pl.multiple_of(n * nc, nc), nc)
                slot_x[:, cols] = dot(sel_near[...], x_near[:, :, cols].reshape(2 * tok, nc)).astype(BF16)

        def pass_on(c):
            if c == X_CHUNKS - 2:
                xp_copies[c].wait_send()
                xp_copies[c + 1].start()
            xp_copies[c].wait_recv()
            fw_copies[c].start()

        def gather(c):
            fw_copies[c].wait_recv()

            @pl.loop(0, d_model // nc)
            def _(n):
                cols = pl.ds(pl.multiple_of(n * nc, nc), nc)
                span = slice(2 * x_cuts[c], 2 * x_cuts[c + 1])
                slot_x[:, cols] += dot(sel_far[:, span], x_far[span, cols]).astype(BF16)

        pass_on(0)
        with jax.named_scope("router"):
            wr_load.wait()
            x = x_near[0]
            w = wr[...]
            w_hi = w.astype(BF16)
            w_rest = w - w_hi.astype(F32)
            w_mid = w_rest.astype(BF16)
            w_lo = (w_rest - w_mid.astype(F32)).astype(BF16)
            logits = dot_bt(x, w_hi) + (dot_bt(x, w_mid) + dot_bt(x, w_lo))
            top = jnp.max(logits, axis=1, keepdims=True)
            prob = jnp.exp(logits - top)
            denom = jnp.sum(prob, axis=1, keepdims=True)
            lane_lo = expert_base(lax.broadcasted_iota(jnp.int32, (tok, experts), 1))
            code_e = code_col[:, 0:experts]
            picked = (code_e >= lane_lo) & (code_e < lane_lo + cap)
            gate = jnp.sum(jnp.where(picked, prob, 0.0), axis=1, keepdims=True) / denom
            gate_col[...] = jnp.broadcast_to(gate, (tok, LANES))

        with jax.named_scope("far0"):
            gather(0)

        pass_at = [0, 1, 3, 4]
        loop_steps = [(5, give, 0, 0), (5, give, 1, 0), (6, give, 0, 1), (7, forward, 0, 0), (7, give, 1, 1), (8, forward, 1, 0), (9, forward, 0, 1), (9, give, 0, 2),
                      (10, forward, 1, 1), (11, forward, 0, 2), (11, give, 1, 2), (13, forward, 1, 2), (14, give, 0, 3)]
        far_at = [x_cuts[c] // (2 * capacity) for c in range(X_CHUNKS)]
        if sent < pack:
            for sub in range(SUBS):
                ex_recv[sub, sent:pack, :] = jnp.zeros((pack - sent, sub_cols), F32)

        with jax.named_scope("experts"):
            for sub in range(SUBS):
                ex_send[sub, 0:8, :] = jnp.zeros((8, sub_cols), F32)
                ex_own[sub, 0:8, :] = jnp.zeros((8, sub_cols), F32)

            @pl.loop(0, local_experts)
            def _(e):
                slot = lax.rem(e, 2)
                @pl.when(e == 0)
                def _():
                    xp_copies[2].start()

                for c in range(1, X_CHUNKS):
                    @pl.when(e == pass_at[c])
                    def _():
                        pass_on(c)

                    @pl.when(e == far_at[c])
                    def _():
                        with jax.named_scope(f"far{c}"):
                            gather(c)

                gate_copy(e, slot).wait()
                up_copy(e, slot).wait()
                rows = slot_x[pl.ds(pl.multiple_of(e * window, window), window), :]
                g = dot_bt(wg[slot], rows)
                u = dot_bt(wu[slot], rows)
                hidden = (jax.nn.silu(g) * u).astype(BF16)

                @pl.when(e + 2 < local_experts)
                def _():
                    gate_copy(e + 2, slot).start()
                    up_copy(e + 2, slot).start()

                down_copy(e, slot).wait()
                row = pl.multiple_of((e * capacity) // 8 * 8, 8)
                for buf, off in ((ex_send, peer_off), (ex_own, own_off)):
                    value = dot_at(hidden, wd[slot, :, pl.ds(off, half)])
                    for sub in range(SUBS):
                        part = value[:, sub * sub_cols:(sub + 1) * sub_cols]
                        buf[sub, pl.ds(row, 8), :] += part[0:8]
                        buf[sub, pl.ds(row + 8, window - 8), :] = part[8:]

                @pl.when(e + 2 < local_experts)
                def _():
                    down_copy(e + 2, slot).start()

                for i in range(groups):
                    @pl.when(e == last_expert[i])
                    def _():
                        yex_copy(0, i).start()
                        if i < EARLY_GROUPS:
                            yex_copy(1, i).start()

                for when, action, sub, i in loop_steps:
                    @pl.when(e == when)
                    def _():
                        action(sub, i)

            for i in range(EARLY_GROUPS, groups):
                yex_copy(1, i).start()

    pl.run_scoped(routed_phase, pltpu.VMEM((slots, 2 * tok), BF16), pltpu.VMEM((slots, 2 * tok), BF16),
                  pltpu.VMEM((2, ff_expert, d_model), BF16), pltpu.VMEM((2, ff_expert, d_model), BF16),
                  pltpu.VMEM((2, ff_expert, d_model), BF16), pltpu.SemaphoreType.DMA((2,)), pltpu.SemaphoreType.DMA((2,)), pltpu.SemaphoreType.DMA((2,)))

    with jax.named_scope("fin_shared"):
        for copy in xp_copies[:-2] + xp_copies[-1:] + fw_copies:
            copy.wait_send()
        res_load.wait()
        for r in range(ROW_BLOCKS):
            if r > 0:
                ysh_copy(r, 0).wait()

            @pl.loop(0, n_half)
            def _(j):
                if r == 0:
                    ysh_copy(r, j).wait()
                cols = pl.ds(pl.multiple_of(j * WIDE, WIDE), WIDE)
                rows = slice(r * r_rows, (r + 1) * r_rows)
                sh_own[j, rows, :] = res_half[rows, cols].astype(F32) + (sh_own[j, rows, :] + sh_recv[r, j])

    def combine(pick, sub, i):
        n = bounds[i + 1] - bounds[i]
        lanes = slice(ep_size * bounds[i], ep_size * bounds[i + 1])
        if sub == 0:
            lane = lax.broadcasted_iota(jnp.int32, (tok, ep_size * n), 1)
            owner = sum((lane >= q * n).astype(jnp.int32) for q in range(1, ep_size))
            lane_code = (lane + owner * (pack - n) + bounds[i]).astype(F32)
            pick[:, lanes] = (code_col[:, 0:1] == lane_code).astype(F32).astype(BF16)
        ret_copy(sub, i, me, rs_send, rs_recv, sib_dev).wait()
        ret_copy(sub, i, xp, rf_send, rf_recv, sib_dev).wait()
        rows = ret[sub, :, bounds[i]:bounds[i + 1], :].reshape(ep_size * n, sub_cols)
        gate = gate_col[:, 0:1]
        for j in range(sub_blocks):
            jj = sub * sub_blocks + j
            sh_own[jj] = sh_own[jj] + gate * dot(pick[:, lanes], rows[:, j * WIDE:(j + 1) * WIDE])

    def out_copies(sub):
        src = out_half.at[sub]
        dst = o_hbm.at[:, pl.ds(pl.multiple_of(own_off + sub * sub_cols, sub_cols), sub_cols)]
        return remote(src, dst, yo_send.at[sub], yo_recv.at[sub], y_peer), pltpu.make_async_copy(src, dst, lo_sem.at[sub])

    def emit(sub):
        for j in range(sub_blocks):
            out_half[sub, :, j * WIDE:(j + 1) * WIDE] = sh_own[sub * sub_blocks + j].astype(BF16)

    def start_out(sub):
        for copy in out_copies(sub):
            copy.start()

    def return_phase(pick):
        steps = [(combine, 0, 0), (combine, 1, 0), (combine, 0, 1), (combine, 1, 1), (combine, 0, 2), (combine, 1, 2), (give, 1, 3), (forward, 0, 3),
                 (combine, 0, 3), (forward, 1, 3), (give, 0, 4), (combine, 1, 3), (forward, 0, 4), (give, 0, 5), (combine, 0, 4), (forward, 0, 5),
                 (combine, 0, 5), (emit, 0), (start_out, 0), (give, 1, 4), (forward, 1, 4), (give, 1, 5), (combine, 1, 4), (forward, 1, 5), (combine, 1, 5), (emit, 1), (start_out, 1)]
        for step in steps:
            with jax.named_scope(step[0].__name__ + "".join(str(a) for a in step[1:])):
                if step[0] is combine:
                    combine(pick, *step[1:])
                else:
                    step[0](*step[1:])

    pl.run_scoped(return_phase, pltpu.VMEM((tok, ep_size * pack), BF16))

    with jax.named_scope("out"):
        for sub in range(SUBS):
            for copy in out_copies(sub):
                copy.wait()


def copy_kernel(src, dst, buf, in_sem, out_sem):
    n = src.shape[0] // COPY_CHUNKS
    reads = [pltpu.make_async_copy(src.at[pl.ds(c * n, n)], buf.at[pl.ds(c * n, n)], in_sem.at[c]) for c in range(COPY_CHUNKS)]
    writes = [pltpu.make_async_copy(buf.at[pl.ds(c * n, n)], dst.at[pl.ds(c * n, n)], out_sem.at[c]) for c in range(COPY_CHUNKS)]
    for copy in reads:
        copy.start()
    for read, write in zip(reads, writes):
        read.wait()
        write.start()
    for copy in writes:
        copy.wait()


def solution(mesh):
    ep_size = mesh.shape["ep"]
    tok_spec = P(("dp", "ep"), None)
    id_spec = P(("dp", "ep"))

    def device_step(normed, residual, w_router, ws_gate, ws_up, ws_down, we_gate, we_up, we_down, first_id, alt_id):
        tok, d_model = normed.shape
        local_experts, _, ff_expert = we_gate.shape
        experts = local_experts * ep_size
        capacity = (5 * tok * ep_size + 4 * experts - 1) // (4 * experts)
        window = -(-(capacity + 7) // 16) * 16
        pack = -(-local_experts * capacity // 16) * 16
        pack_buf = max(pack, (local_experts - 1) * capacity // 8 * 8 + window)
        bounds = [0] + [int(pack * f) // 32 * 32 for f in (0.13, 0.255, 0.4, 0.64, 0.84)] + [pack]
        half = d_model // 2
        slots = local_experts * window
        n_half = half // WIDE
        r_rows = tok // ROW_BLOCKS
        sub_cols = half // SUBS
        dma = pltpu.SemaphoreType.DMA
        any_spec = pl.BlockSpec(memory_space=pl.ANY)
        vmem_spec = pl.BlockSpec(memory_space=pltpu.VMEM)
        per_ret = dma((SUBS, len(bounds) - 1))
        out = pl.pallas_call(
            functools.partial(moe_kernel, (experts, capacity, window, pack, bounds, local_experts, ep_size)),
            out_shape=jax.ShapeDtypeStruct((tok, d_model), BF16),
            in_specs=[any_spec] * 9 + [vmem_spec] * 2,
            out_specs=any_spec,
            scratch_shapes=[
                pltpu.VMEM((2, tok, d_model), BF16),
                pltpu.VMEM((2 * tok, d_model), BF16),
                pltpu.VMEM((tok, d_model), BF16),
                pltpu.VMEM((ep_size, 8, tok), jnp.int32),
                pltpu.VMEM((ep_size, 8, tok), F32),
                pltpu.VMEM((tok, LANES), F32),
                pltpu.VMEM((tok, LANES), F32),
                pltpu.VMEM((slots, d_model), BF16),
                pltpu.VMEM((n_half, tok, WIDE), F32),
                pltpu.VMEM((ROW_BLOCKS, n_half, r_rows, WIDE), F32),
                pltpu.VMEM((ROW_BLOCKS, n_half, r_rows, WIDE), F32),
                pltpu.VMEM((SUBS, pack_buf, sub_cols), F32),
                pltpu.VMEM((SUBS, pack_buf, sub_cols), F32),
                pltpu.VMEM((SUBS, pack, sub_cols), F32),
                pltpu.VMEM((SUBS, ep_size, pack, sub_cols), BF16),
                pltpu.VMEM((SUBS, tok, sub_cols), BF16),
                pltpu.VMEM((tok, half), BF16),
                pltpu.VMEM((experts, d_model), F32),
                dma((ROW_BLOCKS + 2,)), dma((3,)), dma((3,)), dma((1,)), dma((1,)), dma((X_CHUNKS,)), dma((X_CHUNKS,)), dma((X_CHUNKS,)), dma((X_CHUNKS,)),
                dma((ROW_BLOCKS, n_half)), dma((ROW_BLOCKS, n_half)), per_ret, per_ret, per_ret, per_ret, per_ret, per_ret, per_ret, per_ret,
                dma((SUBS,)), dma((SUBS,)), dma((SUBS,)),
            ],
            compiler_params=pltpu.CompilerParams(collective_id=0, has_side_effects=True, vmem_limit_bytes=67043328),
        )(normed, residual, w_router.T, ws_gate, ws_up, ws_down, jnp.swapaxes(we_gate, 1, 2), jnp.swapaxes(we_up, 1, 2), we_down,
          first_id.reshape(1, tok), alt_id.reshape(1, tok))
        return pl.pallas_call(
            copy_kernel,
            out_shape=jax.ShapeDtypeStruct((tok, d_model), BF16),
            in_specs=[any_spec],
            out_specs=any_spec,
            scratch_shapes=[pltpu.VMEM((tok, d_model), BF16), dma((COPY_CHUNKS,)), dma((COPY_CHUNKS,))],
        )(out)

    return jax.shard_map(device_step, mesh=mesh, in_specs=(tok_spec, tok_spec, P(None, None), P(None, 'tp'), P(None, 'tp'), P('tp', None), P('ep', None, 'tp'), P('ep', None, 'tp'), P('ep', 'tp', None), id_spec, id_spec), out_specs=tok_spec, check_vma=False)
```

profile of v0, /device:TPU:0, one launch (start us, length us, event | category | flops | bytes accessed | tf_op | source)
XLA Modules:
  0.0 144.6 jit_solution(1988039626878654384)
XLA Ops:
  0.0 142.1 %shard_map.109.src = bf16[512,2048]{1,0:T(8,128)(2,1)} custom-call(bf16[512,2048]{1,0:T(8,128)(2,1)} %x_hbm.1, bf16[512,2048]{1,0:T(8,128)(2,1)} %res_hbm.1, f32[60,2048]{1,0:T(8,128)} %bitcast.7, bf16[2048,2816]{1,0:T(8,128)(2,1)} %wsg_hbm.1, bf16[2048,2816]{1,0:T(8,128)(2,1)} %wsu_hbm.1, bf16[2816,2048]{1,0:T(8,128)(2,1)} %wsd_hbm.1, ...), custom_call_target="tpu_custom_call" | custom-call | tf_op jit(solution)/shard_map/pallas_call | solution.py:571
  142.1 2.4 %shard_map.110 = bf16[512,2048]{1,0:T(8,128)(2,1)} custom-call(bf16[512,2048]{1,0:T(8,128)(2,1)} %shard_map.109.src), custom_call_target="tpu_custom_call" | custom-call | tf_op jit(solution)/shard_map/pallas_call | solution.py:602
where the time goes:
time: 145 us
  Pallas kernels  144 us (99%)
    pallas_call x1, Pallas kernels, device_step(): pl.pallas_call(functools.partial(moe_kernel, (experts, capacity, window,...  142 us

commit v1 on v0

--- a/solution.py
+++ b/solution.py
@@ -15,7 +15,7 @@
 X_SPLIT = (0, 192, 320, 448, 512)
 X_CHUNKS = 4
 WIDE = 512
-COPY_CHUNKS = 4
+COPY_CHUNKS = 8
 ROW_BLOCKS = 2
 COL = 256
 SUBS = 2
@@ -558,7 +558,7 @@
         window = -(-(capacity + 7) // 16) * 16
         pack = -(-local_experts * capacity // 16) * 16
         pack_buf = max(pack, (local_experts - 1) * capacity // 8 * 8 + window)
-        bounds = [0] + [int(pack * f) // 32 * 32 for f in (0.13, 0.255, 0.4, 0.64, 0.84)] + [pack]
+        bounds = [0] + [int(pack * f) // 32 * 32 for f in (0.13, 0.255, 0.4, 0.6, 0.84)] + [pack]
         half = d_model // 2
         slots = local_experts * window
         n_half = half // WIDE

time: 145 us -> 145 us (level)
  no operation moved by 1% of the time
where the time goes in v1:
time: 145 us
  Pallas kernels  144 us (99%)
    pallas_call x1, Pallas kernels, device_step(): pl.pallas_call(functools.partial(moe_kernel, (experts, capacity, window,...  142 us

profile of v1, /device:TPU:0, one launch (start us, length us, event | category | flops | bytes accessed | tf_op | source)
XLA Modules:
  0.0 144.6 jit_solution(12208767250135277842)
XLA Ops:
  0.0 142.1 %shard_map.109.src = bf16[512,2048]{1,0:T(8,128)(2,1)} custom-call(bf16[512,2048]{1,0:T(8,128)(2,1)} %x_hbm.1, bf16[512,2048]{1,0:T(8,128)(2,1)} %res_hbm.1, f32[60,2048]{1,0:T(8,128)} %bitcast.7, bf16[2048,2816]{1,0:T(8,128)(2,1)} %wsg_hbm.1, bf16[2048,2816]{1,0:T(8,128)(2,1)} %wsu_hbm.1, bf16[2816,2048]{1,0:T(8,128)(2,1)} %wsd_hbm.1, ...), custom_call_target="tpu_custom_call" | custom-call | tf_op jit(solution)/shard_map/pallas_call | solution.py:571
  142.1 2.4 %shard_map.110 = bf16[512,2048]{1,0:T(8,128)(2,1)} custom-call(bf16[512,2048]{1,0:T(8,128)(2,1)} %shard_map.109.src), custom_call_target="tpu_custom_call" | custom-call | tf_op jit(solution)/shard_map/pallas_call | solution.py:602
